TPU v7x, 32 devices: a whole 2x2x4 slice. The times are simulated.
32 devices in a mesh: feat: 4 (over y, core), dom: 8 (over z, x).
Axes of the slice: x: 2, y: 2, z: 4, core: 2. Of those that a mesh axis runs over, the one named last changes fastest.
Arguments:
- features: bfloat16 [32768, 128], P('dom'), may hold values from -6 to 6
- w_input: bfloat16 [128, 256], P(None, 'feat'), may hold values from -0.5 to 0.5
- layer_weights: bfloat16 [4, 256, 256], replicated, may hold values from -0.375 to 0.375
- history: bfloat16 [4, 32768, 256], P(None, 'dom', 'feat'), may hold values from 0 to 2
- tile_values: bfloat16 [256, 6, 128, 128], P('dom'), may hold values from -0.21875 to 0.21875
- tile_columns: int32 [256, 6], P('dom'), may hold values from 0 to 63, as said below
- send_rows: int32 [8, 8, 512], P('dom'), may hold values from 0 to 4095
- send_counts: int32 [8, 8], P('dom'), may hold values from 0 to 512, as said below
Outputs:
- pushed: bfloat16 [4, 32768, 256], P(None, 'dom', 'feat')
- final_rows: bfloat16 [32768, 256], P('dom', 'feat')
Inputs may be any that keep to these rules, and one draw needn't show every extreme that they name: `tile_columns`: per row of tiles the first 2 entries lie below 4096 / 128 (own rows), the others at or above it (halo slots); every halo column tile of every partition is named somewhere. `send_counts`: A partition sends nothing to itself; in every draw some destination receives exactly 512 rows from every other partition.
All inputs are finite; a program needn't handle non-finite values.
Results may differ from a plain program's by a relative error of at most 0.0052.
Values may be sent and summed in bfloat16 or wider, within the bound.
A program may use at most 128 MiB of HBM per device.

v0:
```python
import math
import jax
import jax.numpy as jnp
from jax import lax
from jax.sharding import PartitionSpec as P

LAYERS = 4
ALPHA = 0.1
LAMBDA_DECAY = 0.5


def propagate(own_rows, halo_rows, values, columns, tile_size):
    slice_width = own_rows.shape[1]
    combined = jnp.concatenate([own_rows, halo_rows], axis=0)
    tile_count = combined.shape[0] // tile_size
    flat_tiles = combined.reshape(tile_count, tile_size * slice_width)
    row_tiles, per_row = columns.shape
    selector = (
        columns.reshape(row_tiles * per_row, 1) == jnp.arange(tile_count, dtype=jnp.int32)[None, :]
    ).astype(jnp.bfloat16)
    picked = jnp.dot(selector, flat_tiles, preferred_element_type=jnp.float32).astype(jnp.bfloat16)
    picked = picked.reshape(row_tiles, per_row, tile_size, slice_width)
    summed = jnp.einsum("rkab,rkbf->raf", values, picked, preferred_element_type=jnp.float32)
    return summed.reshape(own_rows.shape[0], slice_width)


def on_device(
    features, w_input, layer_weights, history, tile_values, tile_columns, send_rows, send_counts
):
    initial = jnp.maximum(
        jnp.dot(features, w_input, preferred_element_type=jnp.float32), 0.0
    ).astype(jnp.bfloat16)
    nodes_local, slice_width = initial.shape
    peer_count = send_rows.shape[1]
    slot_count = send_rows.shape[2]
    tile_size = tile_values.shape[-1]
    targets = send_rows[0]
    live_slots = (jnp.arange(slot_count)[None, :] < send_counts[0][:, None])[:, :, None]
    zero_value = jnp.zeros((), jnp.bfloat16)
    halo_list = [
        lax.all_to_all(
            jnp.where(live_slots, history[level][targets], zero_value),
            "dom",
            split_axis=0,
            concat_axis=0,
            tiled=True,
        ).reshape(peer_count * slot_count, slice_width)
        for level in range(LAYERS)
    ]
    pushed = []
    current = initial
    for layer_index in range(LAYERS):
        beta_layer = math.log(LAMBDA_DECAY / (layer_index + 1) + 1.0)
        weight = layer_weights[layer_index]
        aggregated = propagate(
            current, halo_list[layer_index], tile_values, tile_columns, tile_size
        )
        blended = ((1.0 - ALPHA) * aggregated + ALPHA * initial.astype(jnp.float32)).astype(
            jnp.bfloat16
        )
        blended = lax.optimization_barrier(blended)
        pushed.append(current)
        feat_index = lax.axis_index("feat")
        weight_cols = lax.dynamic_slice_in_dim(weight, feat_index * slice_width, slice_width, 1)
        product = jnp.dot(
            lax.all_gather(blended, "feat", axis=1, tiled=True),
            weight_cols,
            preferred_element_type=jnp.float32,
        )
        fresh = jnp.maximum(
            (1.0 - beta_layer) * blended.astype(jnp.float32) + beta_layer * product, 0.0
        )
        current = fresh.astype(jnp.bfloat16)
    return (jnp.stack(pushed), current)


def solution(mesh):
    placed = (
        P("dom", None),
        P(None, "feat"),
        P(),
        P(None, "dom", "feat"),
        P("dom", None, None, None),
        P("dom", None),
        P("dom", None, None),
        P("dom", None),
    )
    return jax.shard_map(
        on_device,
        mesh=mesh,
        in_specs=placed,
        out_specs=(P(None, "dom", "feat"), P("dom", "feat")),
        check_vma=False,
    )
```

profile of v0, /device:TPU:0, one launch (start us, length us, event | category | flops | bytes accessed | tf_op | source)
XLA Modules:
  0.0 316.9 jit_solution(15745469783871784883)
XLA Ops:
  7.2 2.8 fusion.42
  10.0 0.5 copy.80
  10.5 15.0 %gather_fusion = bf16[4096,64]{1,0:T(8,128)(2,1)} fusion(bf16[4096,64]{1,0:T(8,128)(2,1)S(1)} %bitcast.113, s32[4096]{0:T(1024)S(1)} %broadcast_clamp_fusion), kind=kCustom, calls=%fused_computation | custom fusion | bytes 1064960 | tf_op jit(solution)/shard_map/gather | solution.py:42
  25.5 1.5 copy.49
  27.1 0.5 copy.81
  27.6 15.0 %gather_fusion.1 = bf16[4096,64]{1,0:T(8,128)(2,1)} fusion(bf16[4096,64]{1,0:T(8,128)(2,1)S(1)} %bitcast.115, s32[4096]{0:T(1024)S(1)} %broadcast_clamp_fusion), kind=kCustom, calls=%fused_computation.1 | custom fusion | bytes 1064960 | tf_op jit(solution)/shard_map/gather | solution.py:42
  42.6 1.5 copy.55
  44.2 1.5 copy.82
  45.7 15.0 %gather_fusion.2 = bf16[4096,64]{1,0:T(8,128)(2,1)} fusion(bf16[4096,64]{1,0:T(8,128)(2,1)S(1)} %bitcast.116, s32[4096]{0:T(1024)S(1)} %broadcast_clamp_fusion), kind=kCustom, calls=%fused_computation.2 | custom fusion | bytes 1064960 | tf_op jit(solution)/shard_map/gather | solution.py:42
  60.7 2.4 copy.61
  63.1 1.5 copy.83
  64.6 15.0 %gather_fusion.3 = bf16[4096,64]{1,0:T(8,128)(2,1)} fusion(bf16[4096,64]{1,0:T(8,128)(2,1)S(1)} %bitcast.114, s32[4096]{0:T(1024)S(1)} %broadcast_clamp_fusion), kind=kCustom, calls=%fused_computation.3 | custom fusion | bytes 1064960 | tf_op jit(solution)/shard_map/gather | solution.py:42
  79.7 1.5 copy.67
  81.2 0.1 iota_compare_fusion.5
  81.3 2.4 broadcast_select_fusion
  83.7 7.3 %all-to-all-start = ((bf16[8,512,64]{1,2,0:T(8,128)(2,1)}), bf16[8,512,64]{1,2,0:T(8,128)(2,1)S(1)}, u32[]{:S(2)}, u32[]{:S(2)}) async-start(bf16[8,512,64]{1,2,0:T(8,128)(2,1)} %get-tuple-element.13), calls=%async_computation | async-start | bytes 1048576 | tf_op jit(solution)/shard_map/all_to_all | solution.py:41
  91.0 0.1 copy.47
  91.1 0.1 eq.8
  91.3 0.5 fusion.12
  91.7 13.7 %all-to-all-done = bf16[8,512,64]{1,2,0:T(8,128)(2,1)S(1)} async-done(((bf16[8,512,64]{1,2,0:T(8,128)(2,1)}), bf16[8,512,64]{1,2,0:T(8,128)(2,1)S(1)}, u32[]{:S(2)}, u32[]{:S(2)}) %all-to-all-start) | async-done | bytes 524320 | tf_op jit(solution)/shard_map/all_to_all | solution.py:41
  105.5 0.1 pad_maximum_fusion.1
  105.6 1.8 copy.51
  107.4 3.3 %reshape.114 = bf16[64,8192]{1,0:T(8,128)(2,1)S(1)} reshape(bf16[8192,64]{1,0:T(8,128)(2,1)} %copy.51) | data formatting | bytes 2097152 | tf_op jit(solution)/shard_map/reshape | solution.py:16
  110.7 2.7 convolution_convert_fusion.3
  113.4 9.7 %reshape.115 = bf16[32,6,128,64]{3,2,1,0:T(8,128)(2,1)} reshape(bf16[192,8192]{1,0:T(8,128)(2,1)} %convolution_convert_fusion.3) | data formatting | bytes 6291456 | tf_op jit(solution)/shard_map/reshape | solution.py:22
  123.1 6.8 %fusion.14 = f32[32,8,8,128]{3,2,1,0:T(8,128)S(1)} fusion(bf16[32,6,128,64]{3,2,1,0:T(8,128)(2,1)} %reshape.115, bf16[32,6,128,128]{3,2,1,0:T(8,128)(2,1)} %param.12), kind=kOutput, calls=%fused_computation.32 | convolution fusion | flops 402915328 | bytes 10485760 | tf_op jit(solution)/shard_map/rkab,rkbf->raf/dot_general | solution.py:23
  129.9 0.9 fusion.24
  130.8 3.8 %all-to-all-start.1 = ((bf16[8,512,64]{1,2,0:T(8,128)(2,1)}), bf16[8,512,64]{1,2,0:T(8,128)(2,1)S(1)}, u32[]{:S(2)}, u32[]{:S(2)}) async-start(bf16[8,512,64]{1,2,0:T(8,128)(2,1)} %get-tuple-element.11), calls=%async_computation.1 | async-start | bytes 1048576 | tf_op jit(solution)/shard_map/all_to_all | solution.py:41
  134.6 0.2 all-gather.7.cloned.1.call-start
  134.9 14.4 %all-to-all-done.1 = bf16[8,512,64]{1,2,0:T(8,128)(2,1)S(1)} async-done(((bf16[8,512,64]{1,2,0:T(8,128)(2,1)}), bf16[8,512,64]{1,2,0:T(8,128)(2,1)S(1)}, u32[]{:S(2)}, u32[]{:S(2)}) %all-to-all-start.1) | async-done | bytes 524320 | tf_op jit(solution)/shard_map/all_to_all | solution.py:41
  149.3 3.3 %all-gather.5.cloned.1.call-done = bf16[4096,256]{0,1:T(8,128)(2,1)} async-done(((bf16[4096,64]{0,1:T(8,128)(2,1)}), bf16[4096,256]{0,1:T(8,128)(2,1)}) %all-gather.5.cloned.1.call-update) | async-done | bytes 2097168 | tf_op jit(solution)/shard_map/all_gather | solution.py:66
  152.6 2.2 fusion.11
  154.8 0.1 pad_maximum_fusion.2
  154.9 1.8 copy.57
  156.7 3.3 %reshape.117 = bf16[64,8192]{1,0:T(8,128)(2,1)S(1)} reshape(bf16[8192,64]{1,0:T(8,128)(2,1)} %copy.57) | data formatting | bytes 2097152 | tf_op jit(solution)/shard_map/reshape | solution.py:16
  160.0 2.7 convolution_convert_fusion.2
  162.7 9.7 %reshape.118 = bf16[32,6,128,64]{3,2,1,0:T(8,128)(2,1)} reshape(bf16[192,8192]{1,0:T(8,128)(2,1)} %convolution_convert_fusion.2) | data formatting | bytes 6291456 | tf_op jit(solution)/shard_map/reshape | solution.py:22
  172.4 6.8 %fusion.16 = f32[32,8,8,128]{3,2,1,0:T(8,128)S(1)} fusion(bf16[32,6,128,64]{3,2,1,0:T(8,128)(2,1)} %reshape.118, bf16[32,6,128,128]{3,2,1,0:T(8,128)(2,1)} %param.12), kind=kOutput, calls=%fused_computation.34 | convolution fusion | flops 402915328 | bytes 10485760 | tf_op jit(solution)/shard_map/rkab,rkbf->raf/dot_general | solution.py:23
  179.2 0.9 fusion.23
  180.2 0.1 copy-done.8
  180.2 20.3 %all_to_all.20 = bf16[8,512,64]{1,2,0:T(8,128)(2,1)S(1)} all-to-all(bf16[8,512,64]{1,2,0:T(8,128)(2,1)S(1)} %copy-done.8), channel_id=1, replica_groups=mesh['feat'=4,'dom'=8] {'dom'}, dimensions={0} | all-to-all | bytes 1048576 | tf_op jit(solution)/shard_map/all_to_all | solution.py:41
  200.6 2.2 all-gather.7.cloned.1.call-done
  202.8 2.2 fusion.10
  205.1 0.1 pad_maximum_fusion.3
  205.1 1.8 copy.63
  206.9 3.3 %reshape.120 = bf16[64,8192]{1,0:T(8,128)(2,1)S(1)} reshape(bf16[8192,64]{1,0:T(8,128)(2,1)} %copy.63) | data formatting | bytes 2097152 | tf_op jit(solution)/shard_map/reshape | solution.py:16
  210.2 2.7 convolution_convert_fusion.1
  212.9 9.7 %reshape.121 = bf16[32,6,128,64]{3,2,1,0:T(8,128)(2,1)} reshape(bf16[192,8192]{1,0:T(8,128)(2,1)} %convolution_convert_fusion.1) | data formatting | bytes 6291456 | tf_op jit(solution)/shard_map/reshape | solution.py:22
  222.6 6.8 %fusion.18 = f32[32,8,8,128]{3,2,1,0:T(8,128)S(1)} fusion(bf16[32,6,128,64]{3,2,1,0:T(8,128)(2,1)} %reshape.121, bf16[32,6,128,128]{3,2,1,0:T(8,128)(2,1)} %param.12), kind=kOutput, calls=%fused_computation.36 | convolution fusion | flops 402915328 | bytes 10485760 | tf_op jit(solution)/shard_map/rkab,rkbf->raf/dot_general | solution.py:23
  229.4 0.9 fusion.22
  230.4 0.1 copy-done.7
  230.4 20.3 %all_to_all.21 = bf16[8,512,64]{1,2,0:T(8,128)(2,1)S(1)} all-to-all(bf16[8,512,64]{1,2,0:T(8,128)(2,1)S(1)} %copy-done.7), channel_id=1, replica_groups=mesh['feat'=4,'dom'=8] {'dom'}, dimensions={0} | all-to-all | bytes 1048576 | tf_op jit(solution)/shard_map/all_to_all | solution.py:41
  250.8 2.2 all-gather.9.cloned.1.call-done
  253.1 2.2 fusion.9
  255.3 1.1 pad_maximum_fusion.4
  256.4 2.7 copy.69
  259.1 4.2 %reshape.123 = bf16[64,8192]{1,0:T(8,128)(2,1)} reshape(bf16[8192,64]{1,0:T(8,128)(2,1)} %copy.69) | data formatting | bytes 2097152 | tf_op jit(solution)/shard_map/reshape | solution.py:16
  263.3 3.9 %convolution_convert_fusion = bf16[192,8192]{1,0:T(8,128)(2,1)} fusion(bf16[64,8192]{1,0:T(8,128)(2,1)} %reshape.123, s32[192]{0:T(256)S(1)} %eq.8), kind=kOutput, calls=%fused_computation.4 | convolution fusion | flops 202911744 | bytes 4195072 | tf_op jit(solution)/shard_map/dot_general | solution.py:21
  267.3 9.7 %reshape.124 = bf16[32,6,128,64]{3,2,1,0:T(8,128)(2,1)} reshape(bf16[192,8192]{1,0:T(8,128)(2,1)} %convolution_convert_fusion) | data formatting | bytes 6291456 | tf_op jit(solution)/shard_map/reshape | solution.py:22
  276.9 6.8 %fusion.20 = f32[32,8,8,128]{3,2,1,0:T(8,128)S(1)} fusion(bf16[32,6,128,64]{3,2,1,0:T(8,128)(2,1)} %reshape.124, bf16[32,6,128,128]{3,2,1,0:T(8,128)(2,1)} %param.12), kind=kOutput, calls=%fused_computation.38 | convolution fusion | flops 402915328 | bytes 10485760 | tf_op jit(solution)/shard_map/rkab,rkbf->raf/dot_general | solution.py:23
  283.7 0.9 fusion.21
  284.7 2.7 pad_maximum_fusion
  287.4 19.9 %all-gather.11.cloned.1.call-done = bf16[4096,256]{0,1:T(8,128)(2,1)} async-done(((bf16[4096,64]{0,1:T(8,128)(2,1)}), bf16[4096,256]{0,1:T(8,128)(2,1)}) %all-gather.11.cloned.1.call-update) | async-done | bytes 2097168 | tf_op jit(solution)/shard_map/all_gather | solution.py:66
  307.4 3.0 fusion.8
  (41 shorter events, 0.5 us)
Async XLA Ops:
  7.2 84.1 %copy-start = (bf16[4096,128]{1,0:T(8,128)(2,1)S(1)}, bf16[4096,128]{1,0:T(8,128)(2,1)}, u32[]{:S(2)}) copy-start(bf16[4096,128]{1,0:T(8,128)(2,1)} %param.8) | copy-start | bytes 3145732
  7.2 3.3 %copy-start.11 = (s32[1,8,512]{2,1,0:T(8,128)S(1)}, s32[1,8,512]{2,1,0:T(8,128)}, u32[]{:S(2)}) copy-start(s32[1,8,512]{2,1,0:T(8,128)} %param.14) | copy-start | bytes 49156
  64.6 16.6 %copy-start.13 = (s32[1,8]{1,0:T(1,128)S(1)}, s32[1,8]{1,0:T(1,128)}, u32[]{:S(2)}) copy-start(s32[1,8]{1,0:T(1,128)} %param.15) | copy-start | bytes 100
  81.3 9.7 %copy-start.12 = (s32[32,6]{0,1:T(8,128)S(1)}, s32[32,6]{0,1:T(8,128)}, u32[]{:S(2)}) copy-start(s32[32,6]{0,1:T(8,128)} %param.13) | copy-start | bytes 2308
  81.3 9.9 %copy-start.10 = (bf16[128,64]{0,1:T(8,128)(2,1)S(1)}, bf16[128,64]{0,1:T(8,128)(2,1)}, u32[]{:S(2)}) copy-start(bf16[128,64]{0,1:T(8,128)(2,1)} %param.9) | copy-start | bytes 49156
  83.7 21.8 %all-to-all-start = ((bf16[8,512,64]{1,2,0:T(8,128)(2,1)}), bf16[8,512,64]{1,2,0:T(8,128)(2,1)S(1)}, u32[]{:S(2)}, u32[]{:S(2)}) async-start(bf16[8,512,64]{1,2,0:T(8,128)(2,1)} %get-tuple-element.13), calls=%async_computation | async-start | bytes 1048576 | tf_op jit(solution)/shard_map/all_to_all | solution.py:41
  91.0 61.6 %all-gather.5.cloned.1.call-start = ((), (), s32[]{:S(2)}) async-start(), calls=%async_computation.4 | async-start | bytes 2621440 | tf_op jit(solution)/shard_map/all_gather | solution.py:66
  129.8 5.0 %copy-start.9 = (bf16[4,256,256]{2,1,0:T(8,128)(2,1)S(1)}, bf16[4,256,256]{2,1,0:T(8,128)(2,1)}, u32[]{:S(2)}) copy-start(bf16[4,256,256]{2,1,0:T(8,128)(2,1)} %param.10) | copy-start | bytes 1572868
  130.8 21.8 %copy-start.2 = (bf16[4096,64]{0,1:T(8,128)(2,1)S(1)}, bf16[4096,64]{0,1:T(8,128)(2,1)}, u32[]{:S(2)}) copy-start(bf16[4096,64]{0,1:T(8,128)(2,1)} %fusion.24) | copy-start | bytes 1572868
  130.8 18.4 %all-to-all-start.1 = ((bf16[8,512,64]{1,2,0:T(8,128)(2,1)}), bf16[8,512,64]{1,2,0:T(8,128)(2,1)S(1)}, u32[]{:S(2)}, u32[]{:S(2)}) async-start(bf16[8,512,64]{1,2,0:T(8,128)(2,1)} %get-tuple-element.11), calls=%async_computation.1 | async-start | bytes 1048576 | tf_op jit(solution)/shard_map/all_to_all | solution.py:41
  134.6 68.2 %all-gather.7.cloned.1.call-start = ((), (), s32[]{:S(2)}) async-start(), calls=%async_computation.5 | async-start | bytes 2621440 | tf_op jit(solution)/shard_map/all_gather | solution.py:66
  179.2 1.1 copy-start.8
  180.1 22.7 %copy-start.5 = (bf16[4096,64]{0,1:T(8,128)(2,1)S(1)}, bf16[4096,64]{0,1:T(8,128)(2,1)}, u32[]{:S(2)}) copy-start(bf16[4096,64]{0,1:T(8,128)(2,1)} %fusion.23) | copy-start | bytes 1572868
  180.1 72.9 %all-gather.9.cloned.1.call-start = ((), (), s32[]{:S(2)}) async-start(), calls=%async_computation.6 | async-start | bytes 2621440 | tf_op jit(solution)/shard_map/all_gather | solution.py:66
  229.4 1.1 copy-start.7
  230.3 22.7 %copy-start.3 = (bf16[4096,64]{0,1:T(8,128)(2,1)S(1)}, bf16[4096,64]{0,1:T(8,128)(2,1)}, u32[]{:S(2)}) copy-start(bf16[4096,64]{0,1:T(8,128)(2,1)} %fusion.22) | copy-start | bytes 1572868
  230.3 77.0 %all-gather.11.cloned.1.call-start = ((), (), s32[]{:S(2)}) async-start(), calls=%async_computation.7 | async-start | bytes 2621440 | tf_op jit(solution)/shard_map/all_gather | solution.py:66
  255.3 3.9 %copy-start.6 = (bf16[4096,64]{0,1:T(8,128)(2,1)}, bf16[4096,64]{0,1:T(8,128)(2,1)S(1)}, u32[]{:S(2)}) copy-start(bf16[4096,64]{0,1:T(8,128)(2,1)S(1)} %fusion.9) | copy-start | bytes 1572868
  284.7 22.7 %copy-start.4 = (bf16[4096,64]{0,1:T(8,128)(2,1)S(1)}, bf16[4096,64]{0,1:T(8,128)(2,1)}, u32[]{:S(2)}) copy-start(bf16[4096,64]{0,1:T(8,128)(2,1)} %fusion.21) | copy-start | bytes 1572868
  284.7 25.7 %copy-start.1 = (bf16[4096,128]{1,0:T(8,128)(2,1)S(1)}, bf16[4096,128]{1,0:T(8,128)(2,1)}, u32[]{:S(2)}) copy-start(bf16[4096,128]{1,0:T(8,128)(2,1)} %param.8) | copy-start | bytes 3145732
Sparse Core Ops, SparseCore 0:
  130.9 21.6 all-gather.4
  180.2 22.5 all-gather.6
  230.5 22.5 all-gather.8
  284.8 22.5 all-gather.10
where the time goes:
time: 319 us; the launch traced here: 317 us
  local copies, waits for them, and re-layouts  135 us (42%)
  waiting for transfers between devices  55.9 us (18%)
  matrix products  49.3 us (15%)
  blocking collectives  40.6 us (13%)
  between operations  14.1 us (4%)
  starting transfers between devices  11.4 us (4%)
  other arithmetic  10.3 us (3%)
    gather x8, local copies, waits for them, and re-layouts, on_device(): history[level][targets]  67.1 us
    all_to_all x2, blocking collectives, on_device(): lax.all_to_all(jnp.where(live_slots, history[level][targets], zero_value)...  40.6 us
    reshape x4, local copies, waits for them, and re-layouts, propagate(): picked = picked.reshape(row_tiles, per_row, tile_size, slice_width)  38.7 us
    all_to_all x2, waiting for transfers between devices, on_device(): lax.all_to_all(jnp.where(live_slots, history[level][targets], zero_value)...  28.1 us
    all_gather x4, waiting for transfers between devices, on_device(): lax.all_gather(blended, 'feat', axis=1, tiled=True)  27.7 us
    dot_general x4, matrix products, propagate(): jnp.einsum('rkab,rkbf->raf', values, picked, preferred_element_type=jnp.f...  27.1 us
    reshape x4, local copies, waits for them, and re-layouts, propagate(): flat_tiles = combined.reshape(tile_count, tile_size * slice_width)  14.1 us
    dot_general x4, matrix products, propagate(): jnp.dot(selector, flat_tiles, preferred_element_type=jnp.float32)  12.1 us
  transfers between devices with their start and end apart: 6, of which 6 were waited for; matrix products, arithmetic and copies ran while one was open for 1% of the time, Pallas kernels for 0%

commit v1 on v0

--- a/solution.py
+++ b/solution.py
@@ -63,7 +63,7 @@
         feat_index = lax.axis_index("feat")
         weight_cols = lax.dynamic_slice_in_dim(weight, feat_index * slice_width, slice_width, 1)
         product = jnp.dot(
-            lax.all_gather(blended, "feat", axis=1, tiled=True),
+            jnp.concatenate(lax.all_gather(blended, "feat"), axis=1),
             weight_cols,
             preferred_element_type=jnp.float32,
         )

time: 319 us -> 307 us (0.962)
  matrix products: 49.3 us -> 43.1 us
  local copies, waits for them, and re-layouts: 135 us -> 131 us
    gather x8, local copies, waits for them, and re-layouts: 67.1 us -> 52.3 us  [on_device(): history[level][targets]]
    all_gather x0 -> x4, local copies, waits for them, and re-layouts: none -> 7.2 us  [on_device(): lax.all_gather(blended, 'feat')]
    dot_general x4, matrix products: 9.64 us -> 3.43 us  [on_device(): jnp.dot(jnp.concatenate(lax.all_gather(blended, 'feat'), axis=1), weight_...]
where the time goes in v1:
time: 307 us; the launch traced here: 305 us
  local copies, waits for them, and re-layouts  131 us (43%)
  waiting for transfers between devices  56 us (18%)
  matrix products  43.1 us (14%)
  blocking collectives  40.4 us (13%)
  between operations  14.1 us (5%)
  starting transfers between devices  11.3 us (4%)
  other arithmetic  9.25 us (3%)
    gather x8, local copies, waits for them, and re-layouts, on_device(): history[level][targets]  52.3 us
    all_to_all x2, blocking collectives, on_device(): lax.all_to_all(jnp.where(live_slots, history[level][targets], zero_value)...  40.4 us
    reshape x4, local copies, waits for them, and re-layouts, propagate(): picked = picked.reshape(row_tiles, per_row, tile_size, slice_width)  38.7 us
    all_to_all x2, waiting for transfers between devices, on_device(): lax.all_to_all(jnp.where(live_slots, history[level][targets], zero_value)...  28.1 us
    all_gather x4, waiting for transfers between devices, on_device(): lax.all_gather(blended, 'feat')  27.8 us
    dot_general x4, matrix products, propagate(): jnp.einsum('rkab,rkbf->raf', values, picked, preferred_element_type=jnp.f...  27.1 us
    reshape x4, local copies, waits for them, and re-layouts, propagate(): flat_tiles = combined.reshape(tile_count, tile_size * slice_width)  14.1 us
    dot_general x4, matrix products, propagate(): jnp.dot(selector, flat_tiles, preferred_element_type=jnp.float32)  12.1 us
  transfers between devices with their start and end apart: 6, of which 6 were waited for; matrix products, arithmetic and copies ran while one was open for 1% of the time, Pallas kernels for 0%

profile of v1, /device:TPU:0, one launch (start us, length us, event | category | flops | bytes accessed | tf_op | source)
XLA Modules:
  0.0 305.0 jit_solution(770989398882846970)
XLA Ops:
  7.2 2.8 fusion.42
  10.0 0.5 copy.88
  10.5 12.1 %gather_fusion = bf16[4096,64]{1,0:T(8,128)(2,1)S(1)} fusion(bf16[4096,64]{1,0:T(8,128)(2,1)S(1)} %bitcast.141, s32[4096]{0:T(1024)S(1)} %broadcast_clamp_fusion), kind=kCustom, calls=%fused_computation | custom fusion | bytes 1064960 | tf_op jit(solution)/shard_map/gather | solution.py:42
  22.7 1.1 copy.53
  23.8 1.5 copy.89
  25.3 12.1 %gather_fusion.1 = bf16[4096,64]{1,0:T(8,128)(2,1)S(1)} fusion(bf16[4096,64]{1,0:T(8,128)(2,1)S(1)} %bitcast.143, s32[4096]{0:T(1024)S(1)} %broadcast_clamp_fusion), kind=kCustom, calls=%fused_computation.1 | custom fusion | bytes 1064960 | tf_op jit(solution)/shard_map/gather | solution.py:42
  37.5 1.1 copy.60
  38.6 1.5 copy.90
  40.1 12.1 %gather_fusion.2 = bf16[4096,64]{1,0:T(8,128)(2,1)S(1)} fusion(bf16[4096,64]{1,0:T(8,128)(2,1)S(1)} %bitcast.144, s32[4096]{0:T(1024)S(1)} %broadcast_clamp_fusion), kind=kCustom, calls=%fused_computation.2 | custom fusion | bytes 1064960 | tf_op jit(solution)/shard_map/gather | solution.py:42
  52.3 1.1 copy.67
  53.4 1.5 copy.91
  54.9 12.1 %gather_fusion.3 = bf16[4096,64]{1,0:T(8,128)(2,1)S(1)} fusion(bf16[4096,64]{1,0:T(8,128)(2,1)S(1)} %bitcast.142, s32[4096]{0:T(1024)S(1)} %broadcast_clamp_fusion), kind=kCustom, calls=%fused_computation.3 | custom fusion | bytes 1064960 | tf_op jit(solution)/shard_map/gather | solution.py:42
  67.1 0.3 copy.74
  67.5 2.5 broadcast_select_fusion
  70.0 7.3 %all-to-all-start = ((bf16[8,512,64]{1,2,0:T(8,128)(2,1)}), bf16[8,512,64]{1,2,0:T(8,128)(2,1)S(1)}, u32[]{:S(2)}, u32[]{:S(2)}) async-start(bf16[8,512,64]{1,2,0:T(8,128)(2,1)} %get-tuple-element.13), calls=%async_computation | async-start | bytes 1048576 | tf_op jit(solution)/shard_map/all_to_all | solution.py:41
  77.6 0.5 fusion.12
  78.1 13.7 %all-to-all-done = bf16[8,512,64]{1,2,0:T(8,128)(2,1)S(1)} async-done(((bf16[8,512,64]{1,2,0:T(8,128)(2,1)}), bf16[8,512,64]{1,2,0:T(8,128)(2,1)S(1)}, u32[]{:S(2)}, u32[]{:S(2)}) %all-to-all-start) | async-done | bytes 524320 | tf_op jit(solution)/shard_map/all_to_all | solution.py:41
  91.9 1.8 copy.55
  93.7 3.3 %reshape.138 = bf16[64,8192]{1,0:T(8,128)(2,1)S(1)} reshape(bf16[8192,64]{1,0:T(8,128)(2,1)} %copy.55) | data formatting | bytes 2097152 | tf_op jit(solution)/shard_map/reshape | solution.py:16
  97.0 2.7 convolution_convert_fusion.3
  99.7 9.7 %reshape.139 = bf16[32,6,128,64]{3,2,1,0:T(8,128)(2,1)} reshape(bf16[192,8192]{1,0:T(8,128)(2,1)} %convolution_convert_fusion.3) | data formatting | bytes 6291456 | tf_op jit(solution)/shard_map/reshape | solution.py:22
  109.4 6.8 %fusion.14 = f32[32,8,8,128]{3,2,1,0:T(8,128)S(1)} fusion(bf16[32,6,128,64]{3,2,1,0:T(8,128)(2,1)} %reshape.139, bf16[32,6,128,128]{3,2,1,0:T(8,128)(2,1)} %param.12), kind=kOutput, calls=%fused_computation.36 | convolution fusion | flops 402915328 | bytes 10485760 | tf_op jit(solution)/shard_map/rkab,rkbf->raf/dot_general | solution.py:23
  116.2 0.9 fusion.24
  117.1 3.7 %all-to-all-start.1 = ((bf16[8,512,64]{1,2,0:T(8,128)(2,1)}), bf16[8,512,64]{1,2,0:T(8,128)(2,1)S(1)}, u32[]{:S(2)}, u32[]{:S(2)}) async-start(bf16[8,512,64]{1,2,0:T(8,128)(2,1)} %get-tuple-element.11), calls=%async_computation.1 | async-start | bytes 1048576 | tf_op jit(solution)/shard_map/all_to_all | solution.py:41
  120.8 0.2 all-gather.11.cloned.1.call-start
  121.1 14.4 %all-to-all-done.1 = bf16[8,512,64]{1,2,0:T(8,128)(2,1)S(1)} async-done(((bf16[8,512,64]{1,2,0:T(8,128)(2,1)}), bf16[8,512,64]{1,2,0:T(8,128)(2,1)S(1)}, u32[]{:S(2)}, u32[]{:S(2)}) %all-to-all-start.1) | async-done | bytes 524320 | tf_op jit(solution)/shard_map/all_to_all | solution.py:41
  135.5 0.8 copy.98
  136.3 2.6 all-gather.9.cloned.1.call-done
  138.9 1.8 copy.116
  140.8 0.7 fusion.11
  141.4 0.4 copy-done.7
  141.9 1.8 copy.62
  143.6 3.3 %reshape.143 = bf16[64,8192]{1,0:T(8,128)(2,1)S(1)} reshape(bf16[8192,64]{1,0:T(8,128)(2,1)} %copy.62) | data formatting | bytes 2097152 | tf_op jit(solution)/shard_map/reshape | solution.py:16
  146.9 2.7 convolution_convert_fusion.2
  149.7 9.7 %reshape.144 = bf16[32,6,128,64]{3,2,1,0:T(8,128)(2,1)} reshape(bf16[192,8192]{1,0:T(8,128)(2,1)} %convolution_convert_fusion.2) | data formatting | bytes 6291456 | tf_op jit(solution)/shard_map/reshape | solution.py:22
  159.3 6.8 %fusion.16 = f32[32,8,8,128]{3,2,1,0:T(8,128)S(1)} fusion(bf16[32,6,128,64]{3,2,1,0:T(8,128)(2,1)} %reshape.144, bf16[32,6,128,128]{3,2,1,0:T(8,128)(2,1)} %param.12), kind=kOutput, calls=%fused_computation.38 | convolution fusion | flops 402915328 | bytes 10485760 | tf_op jit(solution)/shard_map/rkab,rkbf->raf/dot_general | solution.py:23
  166.1 1.0 fusion.23
  167.1 20.2 %all_to_all.20 = bf16[8,512,64]{1,2,0:T(8,128)(2,1)S(1)} all-to-all(bf16[8,512,64]{1,2,0:T(8,128)(2,1)S(1)} %get-tuple-element.12), channel_id=1, replica_groups=mesh['feat'=4,'dom'=8] {'dom'}, dimensions={0} | all-to-all | bytes 1048576 | tf_op jit(solution)/shard_map/all_to_all | solution.py:41
  187.3 0.8 copy.100
  188.2 1.6 all-gather.11.cloned.1.call-done
  189.8 1.8 copy.115
  191.6 0.7 fusion.10
  192.3 0.4 copy-done.8
  192.7 1.8 copy.69
  194.5 3.3 %reshape.148 = bf16[64,8192]{1,0:T(8,128)(2,1)S(1)} reshape(bf16[8192,64]{1,0:T(8,128)(2,1)} %copy.69) | data formatting | bytes 2097152 | tf_op jit(solution)/shard_map/reshape | solution.py:16
  197.8 2.7 convolution_convert_fusion.1
  200.5 9.7 %reshape.149 = bf16[32,6,128,64]{3,2,1,0:T(8,128)(2,1)} reshape(bf16[192,8192]{1,0:T(8,128)(2,1)} %convolution_convert_fusion.1) | data formatting | bytes 6291456 | tf_op jit(solution)/shard_map/reshape | solution.py:22
  210.2 6.8 %fusion.18 = f32[32,8,8,128]{3,2,1,0:T(8,128)S(1)} fusion(bf16[32,6,128,64]{3,2,1,0:T(8,128)(2,1)} %reshape.149, bf16[32,6,128,128]{3,2,1,0:T(8,128)(2,1)} %param.12), kind=kOutput, calls=%fused_computation.40 | convolution fusion | flops 402915328 | bytes 10485760 | tf_op jit(solution)/shard_map/rkab,rkbf->raf/dot_general | solution.py:23
  217.0 0.9 fusion.22
  218.0 20.2 %all_to_all.21 = bf16[8,512,64]{1,2,0:T(8,128)(2,1)S(1)} all-to-all(bf16[8,512,64]{1,2,0:T(8,128)(2,1)S(1)} %copy-done.6), channel_id=1, replica_groups=mesh['feat'=4,'dom'=8] {'dom'}, dimensions={0} | all-to-all | bytes 1048576 | tf_op jit(solution)/shard_map/all_to_all | solution.py:41
  238.2 2.4 all-gather.13.cloned.1.call-done
  240.7 1.8 copy.114
  242.5 0.7 fusion.9
  243.1 1.1 pad_maximum_fusion.4
  244.2 2.7 copy.76
  246.9 4.2 %reshape.153 = bf16[64,8192]{1,0:T(8,128)(2,1)} reshape(bf16[8192,64]{1,0:T(8,128)(2,1)} %copy.76) | data formatting | bytes 2097152 | tf_op jit(solution)/shard_map/reshape | solution.py:16
  251.1 3.9 %convolution_convert_fusion = bf16[192,8192]{1,0:T(8,128)(2,1)} fusion(bf16[64,8192]{1,0:T(8,128)(2,1)} %reshape.153, s32[192]{0:T(256)S(1)} %eq.8), kind=kOutput, calls=%fused_computation.4 | convolution fusion | flops 202911744 | bytes 4195072 | tf_op jit(solution)/shard_map/dot_general | solution.py:21
  255.0 9.7 %reshape.154 = bf16[32,6,128,64]{3,2,1,0:T(8,128)(2,1)} reshape(bf16[192,8192]{1,0:T(8,128)(2,1)} %convolution_convert_fusion) | data formatting | bytes 6291456 | tf_op jit(solution)/shard_map/reshape | solution.py:22
  264.7 6.8 %fusion.20 = f32[32,8,8,128]{3,2,1,0:T(8,128)S(1)} fusion(bf16[32,6,128,64]{3,2,1,0:T(8,128)(2,1)} %reshape.154, bf16[32,6,128,128]{3,2,1,0:T(8,128)(2,1)} %param.12), kind=kOutput, calls=%fused_computation.42 | convolution fusion | flops 402915328 | bytes 10485760 | tf_op jit(solution)/shard_map/rkab,rkbf->raf/dot_general | solution.py:23
  271.5 0.9 fusion.21
  272.4 1.6 pad_maximum_fusion
  274.0 21.1 %all-gather.15.cloned.1.call-done = bf16[16384,64]{0,1:T(8,128)(2,1)} async-done(((bf16[4096,64]{0,1:T(8,128)(2,1)}), bf16[16384,64]{0,1:T(8,128)(2,1)}) %all-gather.15.cloned.1.call-update) | async-done | bytes 2097168 | tf_op jit(solution)/shard_map/all_gather | solution.py:66
  295.1 1.8 copy.113
  297.0 1.5 fusion.8
  (45 shorter events, 0.9 us)
Async XLA Ops:
  7.2 70.4 %copy-start = (bf16[4096,128]{1,0:T(8,128)(2,1)S(1)}, bf16[4096,128]{1,0:T(8,128)(2,1)}, u32[]{:S(2)}) copy-start(bf16[4096,128]{1,0:T(8,128)(2,1)} %param.8) | copy-start | bytes 3145732
  7.2 3.3 %copy-start.11 = (s32[1,8,512]{2,1,0:T(8,128)S(1)}, s32[1,8,512]{2,1,0:T(8,128)}, u32[]{:S(2)}) copy-start(s32[1,8,512]{2,1,0:T(8,128)} %param.14) | copy-start | bytes 49156
  54.9 12.5 %copy-start.13 = (s32[1,8]{1,0:T(1,128)S(1)}, s32[1,8]{1,0:T(1,128)}, u32[]{:S(2)}) copy-start(s32[1,8]{1,0:T(1,128)} %param.15) | copy-start | bytes 100
  67.5 9.9 %copy-start.12 = (s32[32,6]{0,1:T(8,128)S(1)}, s32[32,6]{0,1:T(8,128)}, u32[]{:S(2)}) copy-start(s32[32,6]{0,1:T(8,128)} %param.13) | copy-start | bytes 2308
  67.5 10.1 %copy-start.10 = (bf16[128,64]{0,1:T(8,128)(2,1)S(1)}, bf16[128,64]{0,1:T(8,128)(2,1)}, u32[]{:S(2)}) copy-start(bf16[128,64]{0,1:T(8,128)(2,1)} %param.9) | copy-start | bytes 49156
  70.0 21.8 %all-to-all-start = ((bf16[8,512,64]{1,2,0:T(8,128)(2,1)}), bf16[8,512,64]{1,2,0:T(8,128)(2,1)S(1)}, u32[]{:S(2)}, u32[]{:S(2)}) async-start(bf16[8,512,64]{1,2,0:T(8,128)(2,1)} %get-tuple-element.13), calls=%async_computation | async-start | bytes 1048576 | tf_op jit(solution)/shard_map/all_to_all | solution.py:41
  77.3 61.6 %all-gather.9.cloned.1.call-start = ((), (), s32[]{:S(2)}) async-start(), calls=%async_computation.4 | async-start | bytes 2621440 | tf_op jit(solution)/shard_map/all_gather | solution.py:66
  116.2 4.9 %copy-start.9 = (bf16[4,256,256]{2,1,0:T(8,128)(2,1)S(1)}, bf16[4,256,256]{2,1,0:T(8,128)(2,1)}, u32[]{:S(2)}) copy-start(bf16[4,256,256]{2,1,0:T(8,128)(2,1)} %param.10) | copy-start | bytes 1572868
  117.1 18.3 %all-to-all-start.1 = ((bf16[8,512,64]{1,2,0:T(8,128)(2,1)}), bf16[8,512,64]{1,2,0:T(8,128)(2,1)S(1)}, u32[]{:S(2)}, u32[]{:S(2)}) async-start(bf16[8,512,64]{1,2,0:T(8,128)(2,1)} %get-tuple-element.11), calls=%async_computation.1 | async-start | bytes 1048576 | tf_op jit(solution)/shard_map/all_to_all | solution.py:41
  120.8 69.0 %all-gather.11.cloned.1.call-start = ((), (), s32[]{:S(2)}) async-start(), calls=%async_computation.5 | async-start | bytes 2621440 | tf_op jit(solution)/shard_map/all_gather | solution.py:66
  138.9 1.8 copy-start.2
  140.7 1.0 copy-start.7
  167.1 73.6 %all-gather.13.cloned.1.call-start = ((), (), s32[]{:S(2)}) async-start(), calls=%async_computation.6 | async-start | bytes 2621440 | tf_op jit(solution)/shard_map/all_gather | solution.py:66
  189.8 1.8 copy-start.5
  191.6 1.0 copy-start.8
  217.0 1.0 copy-start.6
  217.9 77.2 %all-gather.15.cloned.1.call-start = ((), (), s32[]{:S(2)}) async-start(), calls=%async_computation.7 | async-start | bytes 2621440 | tf_op jit(solution)/shard_map/all_gather | solution.py:66
  240.7 1.8 copy-start.3
  295.1 1.9 copy-start.4
  295.1 3.3 %copy-start.1 = (bf16[4096,128]{1,0:T(8,128)(2,1)S(1)}, bf16[4096,128]{1,0:T(8,128)(2,1)}, u32[]{:S(2)}) copy-start(bf16[4096,128]{1,0:T(8,128)(2,1)} %param.8) | copy-start | bytes 3145732
Sparse Core Ops, SparseCore 0:
  117.3 21.6 all-gather.8
  167.2 22.5 all-gather.10
  218.1 22.5 all-gather.12
  272.5 22.5 all-gather.14
